TPU v7x, 32 devices: a whole 2x2x4 slice. The times are simulated.
32 devices in a mesh: ens: 2 (over y), space: 4 (over z), chan: 2 (over x), sub: 2 (over core).
Axes of the slice: x: 2, y: 2, z: 4, core: 2. Of those that a mesh axis runs over, the one named last changes fastest.
Arguments:
- node_state: bfloat16 [8192, 512], P(('ens', 'space'), ('chan', 'sub')), parts along dimension 0, may hold values from -6 to 6
- norm_gains: float32 [2, 512], replicated, may hold values from 0.25 to 1.75
- norm_shifts: float32 [2, 512], replicated, may hold values from -3 to 3
- query_weight: bfloat16 [512, 512], P(None, 'chan')
- key_weight: bfloat16 [512, 512], P(None, 'chan')
- value_weight: bfloat16 [512, 512], P(None, 'chan'), may hold values from -0.25 to 0.25
- out_weight: bfloat16 [512, 512], replicated, may hold values from -0.25 to 0.25
- ffn_in: bfloat16 [2048, 512], P('chan'), may hold values from -0.25 to 0.25
- ffn_out: bfloat16 [2048, 512], P('chan'), may hold values from -0.125 to 0.125
- live_counts: int32 [4], P('space'), may hold values from 512 to 1024, as said below
- send_rows: int32 [4, 2, 256], P('space'), may hold values from 0 to 1023, as said below
- tile_keys: int32 [32, 12], P('space'), may hold values from 0 to 11, as said below
- tile_bits: int32 [32, 12, 4, 128], P('space'), may hold values from -2147483648 to 2147483647, as said below
Outputs:
- updated: bfloat16 [8192, 512], P(('ens', 'space'), ('chan', 'sub')), parts along dimension 0
There are 2 independent parts, one for each index of `ens`. A program takes and returns all parts, laid end to end along the dimension named above; an argument that names none is the same for every part. Nothing has to cross between parts.
Inputs may be any that keep to these rules, and one draw needn't show every extreme that they name: Partition s has live nodes 0 to live_counts[s] - 1; the first and the last partition are full. send_rows[s, 0] lists nodes of partition s read by its lower neighbour, send_rows[s, 1] those read by its upper neighbour; all are live nodes, and entries may repeat. `tile_keys`: slot 0 of every block names the block itself (its index within the partition); other slots name blocks of the same partition (below 8), of the lower halo (from 8) or of the upper halo (from 10); the first partition names no lower halo and the last no upper halo. `tile_bits`: bit j of word w in column r of a slot says whether query r of the block may attend key 32 w + j of the slot's block (bit 31 is the sign bit); in slot 0 every query's own bit is set. Slots whose words are all zero carry no edges.
All inputs are finite; a program needn't handle non-finite values.
Results may differ from a plain program's by a relative error of at most 0.0095.
Values may be sent and summed in bfloat16 or wider, within the bound.
A program may use at most 64 MiB of HBM per device.

v0:
```python
import math
import jax
import jax.numpy as jnp
from jax import lax
from jax.sharding import PartitionSpec as P

HD = 64
NORM_EPS = 1e-05
NEG_FILL = -1e30


def padded_2(array, sides, width):
    for axis, dim in sides:
        size, length = (lax.axis_size(axis), array.shape[dim])
        up = [(i, (i + 1) % size) for i in range(size - 1)]
        down = [(j, i) for i, j in up]
        last = lax.slice_in_dim(array, length - width, length, axis=dim)
        leading = lax.slice_in_dim(array, 0, width, axis=dim)
        before = lax.ppermute(last, axis, up)
        after = lax.ppermute(leading, axis, down)
        array = jnp.concatenate([before, array, after], axis=dim)
    return array


def normalize_rows(source, gain_row, shift_row):
    row_mean = jnp.mean(source, axis=-1, keepdims=True)
    spread = jnp.mean(source * source, axis=-1, keepdims=True) - row_mean * row_mean
    return (source - row_mean) * lax.rsqrt(spread + NORM_EPS) * gain_row + shift_row


def unpack_allowed(key_bits, key_ids, live_count, tile_size, blocks_own):
    shifts = jnp.arange(32, dtype=jnp.int32)
    expanded = jnp.right_shift(key_bits[..., None, :], shifts[:, None]) & 1
    lead_shape = key_bits.shape[:-2]
    expanded = expanded.reshape(lead_shape + (tile_size, tile_size))
    key_index = key_ids[..., None] * tile_size + jnp.arange(tile_size, dtype=jnp.int32)
    key_live = (key_ids[..., None] >= blocks_own) | (key_index < live_count)
    slot_count = key_ids.shape[-1]
    slot_first = jnp.arange(slot_count, dtype=jnp.int32)[:, None, None] == 0
    diagonal = (
        jnp.arange(tile_size, dtype=jnp.int32)[:, None]
        == jnp.arange(tile_size, dtype=jnp.int32)[None, :]
    )
    own_bit = slot_first & diagonal[None]
    return (expanded == 1) & (key_live[..., None] | own_bit)


def hidden_term(rows, in_piece, out_piece):
    hidden = jax.nn.gelu(
        lax.dot_general(
            rows, in_piece, (((1,), (1,)), ((), ())), preferred_element_type=jnp.float32
        )
    ).astype(jnp.bfloat16)
    return jnp.dot(hidden, out_piece, preferred_element_type=jnp.float32)


def on_device(
    node_state,
    norm_gains,
    norm_shifts,
    query_weight,
    key_weight,
    value_weight,
    out_weight,
    ffn_in,
    ffn_out,
    live_counts,
    send_rows,
    tile_keys,
    tile_bits,
):
    n_chan = lax.axis_size("chan")
    n_sub = lax.axis_size("sub")
    groups = n_chan * n_sub
    chan_at = lax.axis_index("chan")
    sub_at = lax.axis_index("sub")
    node_rank = chan_at * n_sub + sub_at
    node_count = node_state.shape[0]
    tile_size = tile_bits.shape[-1]
    word_count = tile_bits.shape[-2]
    slot_count = tile_keys.shape[1]
    blocks_own = tile_keys.shape[0]
    per_rank = node_count // groups
    head_cols = query_weight.shape[1]
    heads_here = head_cols // HD
    halo_rows = send_rows.shape[-1]
    live_count = live_counts[0]

    def own_half(source):
        step_rows = source.shape[0] // groups
        shaped = source.reshape((n_chan, n_sub, step_rows) + source.shape[1:])
        picked = lax.dynamic_index_in_dim(shaped, sub_at, 1, keepdims=False)
        return picked.reshape((n_chan * step_rows,) + source.shape[1:])

    node_rows = lax.all_to_all(node_state, ("chan", "sub"), split_axis=0, concat_axis=1, tiled=True)
    pair_weight = jnp.concatenate([key_weight, value_weight], axis=1)
    gathered = lax.all_gather(node_state, ("chan", "sub"), axis=1, tiled=True)
    normed = normalize_rows(gathered.astype(jnp.float32), norm_gains[0], norm_shifts[0]).astype(
        jnp.bfloat16
    )
    key_values = jnp.dot(normed, pair_weight, preferred_element_type=jnp.float32).astype(
        jnp.bfloat16
    )
    queries = jnp.dot(own_half(normed), query_weight, preferred_element_type=jnp.float32).astype(
        jnp.bfloat16
    )
    send_list = send_rows.reshape(2 * halo_rows)
    outgoing = jnp.take(key_values, send_list, axis=0)
    padded = padded_2(outgoing, (("space", 0),), halo_rows)
    extended = jnp.concatenate([key_values, padded[:halo_rows], padded[-halo_rows:]], axis=0)
    key_blocks = extended.reshape(-1, tile_size, 2 * head_cols)
    key_ids = own_half(tile_keys)
    key_bits = own_half(tile_bits)
    block_total = key_ids.shape[0]
    per_round = math.gcd(block_total, 4)
    rounds = block_total // per_round
    score_scale = 1.0 / math.sqrt(HD)

    def attend(inputs):
        q_part, id_part, bit_part = inputs
        chosen = key_blocks[id_part]
        keys_part = chosen[..., :head_cols].reshape(
            per_round, slot_count, tile_size, heads_here, HD
        )
        values_part = chosen[..., head_cols:].reshape(
            per_round, slot_count, tile_size, heads_here, HD
        )
        scores = (
            jnp.einsum("grhd,gtkhd->ghrtk", q_part, keys_part, preferred_element_type=jnp.float32)
            * score_scale
        )
        allowed = unpack_allowed(bit_part, id_part, live_count, tile_size, blocks_own)
        allowed = jnp.transpose(allowed, (0, 3, 1, 2))[:, None]
        masked = jnp.where(allowed, scores, NEG_FILL)
        row_max = jnp.max(masked, axis=(3, 4), keepdims=True)
        weights = jnp.where(allowed, jnp.exp(scores - row_max), 0.0)
        row_total = jnp.sum(weights, axis=(3, 4))
        mixed_heads = jnp.einsum(
            "ghrtk,gtkhd->grhd",
            weights.astype(jnp.bfloat16),
            values_part,
            preferred_element_type=jnp.float32,
        )
        mixed_heads = mixed_heads / jnp.transpose(row_total, (0, 2, 1))[..., None]
        return mixed_heads.astype(jnp.bfloat16).reshape(per_round * tile_size, head_cols)

    query_groups = queries.reshape(rounds, per_round, tile_size, heads_here, HD)
    attended = lax.map(
        attend,
        (
            query_groups,
            key_ids.reshape(rounds, per_round, slot_count),
            key_bits.reshape(rounds, per_round, slot_count, word_count, tile_size),
        ),
    )
    mixed_rows = jnp.dot(
        lax.all_to_all(
            attended.reshape(n_chan, per_rank, head_cols),
            "chan",
            split_axis=0,
            concat_axis=2,
            tiled=True,
        )[0],
        out_weight,
        preferred_element_type=jnp.float32,
    )
    after_attn = node_rows.astype(jnp.float32) + mixed_rows
    normed_two = normalize_rows(after_attn, norm_gains[1], norm_shifts[1]).astype(jnp.bfloat16)
    all_rows = lax.all_gather(normed_two, "chan", axis=0, tiled=True)
    update = lax.psum_scatter(
        hidden_term(all_rows, ffn_in, ffn_out).astype(jnp.bfloat16),
        "chan",
        scatter_dimension=0,
        tiled=True,
    ).astype(jnp.float32)
    position = node_rank * per_rank + jnp.arange(per_rank, dtype=jnp.int32)
    result = jnp.where((position < live_count)[:, None], after_attn + update, 0.0).astype(
        jnp.bfloat16
    )
    return lax.all_to_all(result, ("chan", "sub"), split_axis=1, concat_axis=0, tiled=True)


def solution(mesh):
    in_specs = (
        P(("ens", "space"), ("chan", "sub")),
        P(),
        P(),
        P(None, "chan"),
        P(None, "chan"),
        P(None, "chan"),
        P(),
        P("chan", None),
        P("chan", None),
        P("space"),
        P("space", None, None),
        P("space", None),
        P("space", None, None, None),
    )
    out_specs = P(("ens", "space"), ("chan", "sub"))
    return jax.shard_map(
        on_device, mesh=mesh, in_specs=in_specs, out_specs=out_specs, check_vma=False
    )
```

profile of v0, /device:TPU:0, one launch (start us, length us, event | category | flops | bytes accessed | tf_op | source)
XLA Modules:
  0.0 127.1 jit_solution(3869248447497856356)
XLA Ops:
  7.3 4.2 %all-to-all-start = ((bf16[4,256,128]{2,1,0:T(8,128)(2,1)}), bf16[4,256,128]{2,1,0:T(8,128)(2,1)}, u32[]{:S(2)}, u32[]{:S(2)}) async-start(bf16[4,256,128]{2,1,0:T(8,128)(2,1)} %bitcast.86), calls=%async_computation | async-start | bytes 524288 | tf_op jit(solution)/shard_map/all_to_all | solution.py:95
  15.6 1.2 fusion.10
  18.5 10.0 %all-gather.2.cloned.1.call-done = bf16[1024,512]{1,0:T(8,128)(2,1)} async-done(((bf16[1024,128]{1,0:T(8,128)(2,1)}), bf16[1024,512]{1,0:T(8,128)(2,1)}) %all-gather.2.cloned.1.call-update) | async-done | bytes 1048592 | tf_op jit(solution)/shard_map/all_gather | solution.py:97
  28.5 1.6 %convert_reduce_fusion = (f32[1024]{0:T(1024)S(1)}, f32[1024]{0:T(1024)S(1)}) fusion(bf16[1024,512]{1,0:T(8,128)(2,1)} %all-gather.2.cloned.1.call-done), kind=kLoop, calls=%fused_computation.17 | loop fusion | flops 2095104 | bytes 1056768 | tf_op jit(solution)/shard_map/reduce_sum | solution.py:26
  30.1 1.7 %fusion.14 = bf16[1024,512]{1,0:T(8,128)(2,1)S(1)} fusion(bf16[1024,512]{1,0:T(8,128)(2,1)} %all-gather.2.cloned.1.call-done, f32[512]{0:T(512)S(1)} %bitcast.103, f32[512]{0:T(512)S(1)} %bitcast.102, f32[1024]{0:T(1024)S(1)} %get-tuple-element.41, f32[1024]{0:T(1024)S(1)} %get-tuple-element.40), kind=kLoop, calls=%fused_computation.22 | loop fusion | flops 3145728 | bytes 2109440 | tf_op jit(solution)/shard_map/convert_element_type | solution.py:98
  33.5 2.0 %gather_fusion = bf16[512,512]{1,0:T(8,128)(2,1)S(1)} fusion(bf16[1024,512]{1,0:T(8,128)(2,1)S(1)} %convolution_convert_fusion, s32[1024]{0:T(1024)S(1)} %pad_clamp_fusion.1), kind=kCustom, calls=%fused_computation | custom fusion | bytes 1050624 | tf_op jit(solution)/shard_map/jit(_take)/gather | solution.py:108
  35.7 3.4 %collective-permute-start = (bf16[256,512]{1,0:T(8,128)(2,1)S(1)}, bf16[256,512]{1,0:T(8,128)(2,1)S(1)}, u32[]{:S(2)}, u32[]{:S(2)}) collective-permute-start(bf16[256,512]{1,0:T(8,128)(2,1)S(1)} %get-tuple-element.34), channel_id=1, source_target_pairs={{0,4},{4,8},{8,12},{1,5},{5,9},{9,13},{2,6},{6,10},{10,14},{3,7},{... | collective-permute-start | bytes 786440 | tf_op jit(solution)/shard_map/ppermute | solution.py:19
  39.1 1.3 %collective-permute-start.1 = (bf16[256,512]{1,0:T(8,128)(2,1)S(1)}, bf16[256,512]{1,0:T(8,128)(2,1)}, u32[]{:S(2)}, u32[]{:S(2)}) collective-permute-start(bf16[256,512]{1,0:T(8,128)(2,1)S(1)} %get-tuple-element.35), channel_id=1, source_target_pairs={{4,0},{8,4},{12,8},{5,1},{9,5},{13,9},{6,2},{10,6},{14,10},{7,3},{... | collective-permute-start | bytes 786440 | tf_op jit(solution)/shard_map/ppermute | solution.py:20
  40.4 1.1 constant_dynamic-slice_fusion
  42.9 2.2 %collective-permute-done = bf16[256,512]{1,0:T(8,128)(2,1)S(1)} collective-permute-done((bf16[256,512]{1,0:T(8,128)(2,1)S(1)}, bf16[256,512]{1,0:T(8,128)(2,1)S(1)}, u32[]{:S(2)}, u32[]{:S(2)}) %collective-permute-start) | collective-permute-done | bytes 262176 | tf_op jit(solution)/shard_map/ppermute | solution.py:19
  45.7 3.5 %collective-permute-done.1 = bf16[256,512]{1,0:T(8,128)(2,1)} collective-permute-done((bf16[256,512]{1,0:T(8,128)(2,1)S(1)}, bf16[256,512]{1,0:T(8,128)(2,1)}, u32[]{:S(2)}, u32[]{:S(2)}) %collective-permute-start.1) | collective-permute-done | bytes 262176 | tf_op jit(solution)/shard_map/ppermute | solution.py:20
  49.3 1.5 %pad_maximum_fusion = bf16[1536,512]{1,0:T(8,128)(2,1)S(1)} fusion(bf16[256,512]{1,0:T(8,128)(2,1)} %collective-permute-done.1, bf16[256,512]{1,0:T(8,128)(2,1)} %copy-done.5, bf16[1024,512]{1,0:T(8,128)(2,1)} %copy-done.1), kind=kLoop, calls=%fused_computation.32 | loop fusion | flops 4718592 | bytes 3145728 | tf_op jit(solution)/shard_map/concatenate | solution.py:110
  50.8 5.0 %gather_fusion.1 = bf16[48,128,512]{2,1,0:T(8,128)(2,1)} fusion(bf16[12,128,512]{2,1,0:T(8,128)(2,1)S(1)} %bitcast.77, s32[1024]{0:T(1024)S(1)} %pad_clamp_fusion), kind=kCustom, calls=%fused_computation.1 | custom fusion | bytes 12583104 | tf_op jit(solution)/shard_map/while/body/eval_jaxpr/gather | solution.py:121
  55.7 8.6 %copy.29 = bf16[48,128,512]{1,2,0:T(8,128)(2,1)} copy(bf16[48,128,512]{2,1,0:T(8,128)(2,1)} %gather_fusion.1) | data formatting | bytes 12582912 | tf_op jit(solution)/shard_map/while/body/eval_jaxpr/gather | solution.py:121
  64.4 3.6 %fusion.57 = (bf16[4,12,128,256]{2,3,1,0:T(8,128)(2,1)S(1)}, bf16[4,12,128,256]{2,3,1,0:T(8,128)(2,1)S(1)}) fusion(bf16[4,12,128,512]{2,3,1,0:T(8,128)(2,1)} %bitcast.78), kind=kLoop, calls=%fused_computation.83 | loop fusion | bytes 12582912 | tf_op jit(solution)/shard_map/while/body/eval_jaxpr/slice | solution.py:125
  68.0 3.1 %select_reduce_fusion = (f32[4,4,128]{2,1,0:T(4,128)S(1)}, f32[4,4,128,12,128]{2,4,3,1,0:T(8,128)S(1)}) fusion(pred[4,128,12,128]{1,3,2,0:T(8,128)(4,1)S(1)} %bitcast.79, bf16[4,12,128,4,64]{2,4,3,1,0:T(8,128)(2,1)S(1)} %bitcast.83, bf16[4,128,4,64,1]{3,2,1,0,4:T(4,128)(2,1)S(1)} %bitcast.89), kind=kOutput, calls=%fused_computation.3 | convolution fusion | flops 412088320 | bytes 16785408 | tf_op jit(solution)/shard_map/while/body/eval_jaxpr/grhd,gtkhd->ghrtk/dot_general | solution.py:129
  71.1 2.8 %fusion = f32[4,4,128]{2,1,0:T(4,128)S(1)} fusion(f32[4,4,128,12,128]{2,4,3,1,0:T(8,128)S(1)} %get-tuple-element.45, f32[4,4,128]{2,1,0:T(4,128)S(1)} %get-tuple-element.44, pred[4,128,12,128]{1,3,2,0:T(8,128)(4,1)S(1)} %bitcast.80), kind=kLoop, calls=%fused_computation.4 | loop fusion | flops 12580864 | bytes 13385728 | tf_op jit(solution)/shard_map/while/body/eval_jaxpr/reduce_sum | solution.py:137
  73.9 3.4 %fusion.38 = bf16[4,128,4,64]{1,3,2,0:T(8,128)(2,1)S(1)} fusion(f32[4,4,128,12,128]{2,4,3,1,0:T(8,128)S(1)} %get-tuple-element.45, f32[4,4,128]{2,1,0:T(4,128)S(1)} %get-tuple-element.44, pred[4,128,12,128]{1,3,2,0:T(8,128)(4,1)S(1)} %bitcast.81, bf16[4,12,128,4,64]{2,4,3,1,0:T(8,128)(2,1)S(1)} %bitcast.82, f32[4,128,4]{1,2,0:T(4,128)S(1)} %bitcast.93), kind=kOutput, calls=%fused_computation.42 | convolution fusion | flops 415498240 | bytes 16793600 | tf_op jit(solution)/shard_map/while/body/eval_jaxpr/ghrtk,gtkhd->grhd/dot_general | solution.py:138
  77.8 7.6 %all_to_all.47 = bf16[2,256,256]{1,2,0:T(8,128)(2,1)S(1)} all-to-all(bf16[2,256,256]{1,2,0:T(8,128)(2,1)S(1)} %copy.36), channel_id=1, replica_groups=mesh['ens'=2,'space'=4,'chan'=2,'sub'=2] {'chan'}, dimensions={0} | all-to-all | bytes 524288 | tf_op jit(solution)/shard_map/all_to_all | solution.py:157
  85.4 1.4 %fusion.56 = (f32[256]{0:T(256)S(1)}, f32[256]{0:T(256)S(1)}, f32[256,512]{1,0:T(8,128)S(1)}) fusion(bf16[256,512]{0,1:T(8,128)(2,1)S(1)} %bitcast.88, bf16[512,512]{1,0:T(8,128)(2,1)S(1)} %copy-done.4, bf16[4,256,128]{2,1,0:T(8,128)(2,1)} %all-to-all-done), kind=kOutput, calls=%fused_computation.82 | convolution fusion | flops 134872576 | bytes 1574912 | tf_op jit(solution)/shard_map/dot_general | solution.py:156
  87.0 7.0 %all_gather.7 = bf16[512,512]{1,0:T(8,128)(2,1)S(1)} all-gather(bf16[256,512]{1,0:T(8,128)(2,1)S(1)} %add_convert_fusion), channel_id=1, replica_groups=mesh['ens'=2,'space'=4,'chan'=2,'sub'=2] {'chan'}, dimensions={0}, use_global_device_ids=true | all-gather | bytes 786432 | tf_op jit(solution)/shard_map/all_gather | solution.py:169
  94.0 2.3 %convolution_convert_fusion.1 = bf16[512,512]{1,0:T(8,128)(2,1)} fusion(bf16[1024,512]{1,0:T(8,128)(2,1)S(1)} %copy-done, bf16[512,512]{1,0:T(8,128)(2,1)S(1)} %all_gather.7, bf16[1024,512]{1,0:T(8,128)(2,1)S(1)} %copy-done.7), kind=kOutput, calls=%fused_computation.34 | convolution fusion | flops 1078722560 | bytes 3145728 | tf_op jit(solution)/shard_map/dot_general | solution.py:54
  96.3 13.8 %reduce-scatter.2.cloned.1.call-done = bf16[256,512]{1,0:T(8,128)(2,1)} async-done(((bf16[512,512]{1,0:T(8,128)(2,1)}), bf16[256,512]{1,0:T(8,128)(2,1)}) %reduce-scatter.2.cloned.1.call-update) | async-done | bytes 262160 | tf_op jit(solution)/shard_map/reduce_scatter | solution.py:170
  111.2 8.4 %all_to_all.48 = bf16[256,4,128]{2,0,1:T(8,128)(2,1)S(1)} all-to-all(bf16[256,4,128]{2,0,1:T(8,128)(2,1)S(1)} %copy_bitcast_fusion), channel_id=1, replica_groups=mesh['ens'=2,'space'=4,'chan'=2,'sub'=2] {'chan','sub'}, dimensions={1} | all-to-all | bytes 524288 | tf_op jit(solution)/shard_map/all_to_all | solution.py:180
  (59 shorter events, 12.1 us)
Async XLA Ops:
  6.5 87.5 %copy-start = (bf16[1024,512]{1,0:T(8,128)(2,1)S(1)}, bf16[1024,512]{1,0:T(8,128)(2,1)}, u32[]{:S(2)}) copy-start(bf16[1024,512]{1,0:T(8,128)(2,1)} %param.21) | copy-start | bytes 3145732
  6.5 26.2 %copy-start.9 = (bf16[512,256]{1,0:T(8,128)(2,1)S(1)}, bf16[512,256]{1,0:T(8,128)(2,1)}, u32[]{:S(2)}) copy-start(bf16[512,256]{1,0:T(8,128)(2,1)} %param.17) | copy-start | bytes 786436
  6.5 26.2 %copy-start.8 = (bf16[512,256]{1,0:T(8,128)(2,1)S(1)}, bf16[512,256]{1,0:T(8,128)(2,1)}, u32[]{:S(2)}) copy-start(bf16[512,256]{1,0:T(8,128)(2,1)} %param.18) | copy-start | bytes 786436
  6.5 21.9 %all-gather.2.cloned.1.call-start = ((), (), s32[]{:S(2)}) async-start(), calls=%async_computation.4 | async-start | bytes 1310720 | tf_op jit(solution)/shard_map/all_gather | solution.py:97
  7.3 70.6 %all-to-all-start = ((bf16[4,256,128]{2,1,0:T(8,128)(2,1)}), bf16[4,256,128]{2,1,0:T(8,128)(2,1)}, u32[]{:S(2)}, u32[]{:S(2)}) async-start(bf16[4,256,128]{2,1,0:T(8,128)(2,1)} %bitcast.86), calls=%async_computation | async-start | bytes 524288 | tf_op jit(solution)/shard_map/all_to_all | solution.py:95
  11.5 98.6 %reduce-scatter.2.cloned.1.call-start = ((), (), s32[]{:S(2)}) async-start(), calls=%async_computation.5 | async-start | bytes 786432 | tf_op jit(solution)/shard_map/reduce_scatter | solution.py:170
  31.7 1.0 copy-start.2
  33.5 2.2 %copy-start.1 = (bf16[1024,512]{1,0:T(8,128)(2,1)}, bf16[1024,512]{1,0:T(8,128)(2,1)S(1)}, u32[]{:S(2)}) copy-start(bf16[1024,512]{1,0:T(8,128)(2,1)S(1)} %convolution_convert_fusion) | copy-start | bytes 3145732
  35.5 6.0 %copy-start.6 = (bf16[512,256]{1,0:T(8,128)(2,1)S(1)}, bf16[512,256]{1,0:T(8,128)(2,1)}, u32[]{:S(2)}) copy-start(bf16[512,256]{1,0:T(8,128)(2,1)} %param.16) | copy-start | bytes 786436
  35.7 9.3 %collective-permute-start = (bf16[256,512]{1,0:T(8,128)(2,1)S(1)}, bf16[256,512]{1,0:T(8,128)(2,1)S(1)}, u32[]{:S(2)}, u32[]{:S(2)}) collective-permute-start(bf16[256,512]{1,0:T(8,128)(2,1)S(1)} %get-tuple-element.34), channel_id=1, source_target_pairs={{0,4},{4,8},{8,12},{1,5},{5,9},{9,13},{2,6},{6,10},{10,14},{3,7},{... | collective-permute-start | bytes 786440 | tf_op jit(solution)/shard_map/ppermute | solution.py:19
  39.1 10.2 %collective-permute-start.1 = (bf16[256,512]{1,0:T(8,128)(2,1)S(1)}, bf16[256,512]{1,0:T(8,128)(2,1)}, u32[]{:S(2)}, u32[]{:S(2)}) collective-permute-start(bf16[256,512]{1,0:T(8,128)(2,1)S(1)} %get-tuple-element.35), channel_id=1, source_target_pairs={{4,0},{8,4},{12,8},{5,1},{9,5},{13,9},{6,2},{10,6},{14,10},{7,3},{... | collective-permute-start | bytes 786440 | tf_op jit(solution)/shard_map/ppermute | solution.py:20
  45.0 0.7 copy-start.5
  64.4 3.6 %copy-start.3 = (bf16[4,128,4,64]{3,2,1,0:T(4,128)(2,1)S(1)}, bf16[4,128,4,64]{3,2,1,0:T(4,128)(2,1)}, u32[]{:S(2)}) copy-start(bf16[4,128,4,64]{3,2,1,0:T(4,128)(2,1)} %reshape.235) | copy-start | bytes 786436
  73.9 11.5 %copy-start.4 = (bf16[512,512]{1,0:T(8,128)(2,1)S(1)}, bf16[512,512]{1,0:T(8,128)(2,1)}, u32[]{:S(2)}) copy-start(bf16[512,512]{1,0:T(8,128)(2,1)} %param.19) | copy-start | bytes 1572868
  77.4 16.6 %copy-start.7 = (bf16[1024,512]{1,0:T(8,128)(2,1)S(1)}, bf16[1024,512]{1,0:T(8,128)(2,1)}, u32[]{:S(2)}) copy-start(bf16[1024,512]{1,0:T(8,128)(2,1)} %param.20) | copy-start | bytes 3145732
Sparse Core Ops, SparseCore 0:
  8.9 19.5 all-gather.1
  96.4 13.6 reduce-scatter.1
where the time goes:
time: 128 us; the launch traced here: 127 us
  waiting for transfers between devices  30.2 us (24%)
  local copies, waits for them, and re-layouts  28.3 us (22%)
  blocking collectives  23 us (18%)
  between operations  14.3 us (11%)
  other arithmetic  11.2 us (9%)
  matrix products  11.2 us (9%)
  starting transfers between devices  8.95 us (7%)
    reduce_scatter x1, waiting for transfers between devices, on_device(): lax.psum_scatter(hidden_term(all_rows, ffn_in, ffn_out).astype(jnp.bfloat...  13.8 us
    gather x2, local copies, waits for them, and re-layouts, attend(): chosen = key_blocks[id_part]  13.6 us
    all_gather x1, waiting for transfers between devices, on_device(): gathered = lax.all_gather(node_state, ('chan', 'sub'), axis=1, tiled=True)  10 us
    all_to_all x1, blocking collectives, on_device(): lax.all_to_all(result, ('chan', 'sub'), split_axis=1, concat_axis=0, tile...  8.39 us
    all_to_all x1, blocking collectives, on_device(): lax.all_to_all(attended.reshape(n_chan, per_rank, head_cols), 'chan', spl...  7.56 us
    all_gather x1, blocking collectives, on_device(): all_rows = lax.all_gather(normed_two, 'chan', axis=0, tiled=True)  7.04 us
    all_to_all x1, starting transfers between devices, on_device(): lax.all_to_all(node_state, ('chan', 'sub'), split_axis=0, concat_axis=1,...  4.25 us
    unnamed x23, local copies, waits for them, and re-layouts  3.83 us
  transfers between devices with their start and end apart: 5, of which 4 were waited for; matrix products, arithmetic and copies ran while one was open for 34% of the time, Pallas kernels for 0%

commit v1 on v0

--- a/solution.py
+++ b/solution.py
@@ -3,10 +3,18 @@
 import jax.numpy as jnp
 from jax import lax
 from jax.sharding import PartitionSpec as P
+from jax.lax import all_to_all, psum
 
 HD = 64
 NORM_EPS = 1e-05
 NEG_FILL = -1e30
+
+
+def choose_the_stocks(row_data, net_axis, ndim_at, k_dim):
+    latest = psum(1, net_axis)
+    v_now = jnp.split(row_data, latest, ndim_at)
+    s_next = jnp.stack(v_now, 0)
+    return jnp.concatenate(all_to_all(s_next, net_axis, 0, 0), k_dim)
 
 
 def padded_2(array, sides, width):
@@ -177,7 +185,7 @@
     result = jnp.where((position < live_count)[:, None], after_attn + update, 0.0).astype(
         jnp.bfloat16
     )
-    return lax.all_to_all(result, ("chan", "sub"), split_axis=1, concat_axis=0, tiled=True)
+    return choose_the_stocks(result, ("chan", "sub"), 1, 0)
 
 
 def solution(mesh):

time: 128 us -> 128 us (level)
  no operation moved by 1% of the time
where the time goes in v1:
time: 128 us; the launch traced here: 127 us
  waiting for transfers between devices  30.2 us (24%)
  local copies, waits for them, and re-layouts  28.3 us (22%)
  blocking collectives  23 us (18%)
  between operations  14.4 us (11%)
  other arithmetic  11.2 us (9%)
  matrix products  11.2 us (9%)
  starting transfers between devices  8.95 us (7%)
    reduce_scatter x1, waiting for transfers between devices, on_device(): lax.psum_scatter(hidden_term(all_rows, ffn_in, ffn_out).astype(jnp.bfloat...  13.8 us
    gather x2, local copies, waits for them, and re-layouts, attend(): chosen = key_blocks[id_part]  13.6 us
    all_gather x1, waiting for transfers between devices, on_device(): gathered = lax.all_gather(node_state, ('chan', 'sub'), axis=1, tiled=True)  10 us
    all_to_all x1, blocking collectives, choose_the_stocks(): return jnp.concatenate(all_to_all(s_next, net_axis, 0, 0), k_dim)  8.39 us
    all_to_all x1, blocking collectives, on_device(): lax.all_to_all(attended.reshape(n_chan, per_rank, head_cols), 'chan', spl...  7.56 us
    all_gather x1, blocking collectives, on_device(): all_rows = lax.all_gather(normed_two, 'chan', axis=0, tiled=True)  7.04 us
    all_to_all x1, starting transfers between devices, on_device(): lax.all_to_all(node_state, ('chan', 'sub'), split_axis=0, concat_axis=1,...  4.25 us
    unnamed x23, local copies, waits for them, and re-layouts  3.82 us
  transfers between devices with their start and end apart: 5, of which 4 were waited for; matrix products, arithmetic and copies ran while one was open for 34% of the time, Pallas kernels for 0%

profile of v1, /device:TPU:0, one launch (start us, length us, event | category | flops | bytes accessed | tf_op | source)
XLA Modules:
  0.0 127.2 jit_solution(5159760793971322)
XLA Ops:
  7.3 4.2 %all-to-all-start = ((bf16[4,256,128]{2,1,0:T(8,128)(2,1)}), bf16[4,256,128]{2,1,0:T(8,128)(2,1)}, u32[]{:S(2)}, u32[]{:S(2)}) async-start(bf16[4,256,128]{2,1,0:T(8,128)(2,1)} %bitcast.87), calls=%async_computation | async-start | bytes 524288 | tf_op jit(solution)/shard_map/all_to_all | solution.py:103
  15.6 1.2 fusion.10
  18.5 10.0 %all-gather.2.cloned.1.call-done = bf16[1024,512]{1,0:T(8,128)(2,1)} async-done(((bf16[1024,128]{1,0:T(8,128)(2,1)}), bf16[1024,512]{1,0:T(8,128)(2,1)}) %all-gather.2.cloned.1.call-update) | async-done | bytes 1048592 | tf_op jit(solution)/shard_map/all_gather | solution.py:105
  28.5 1.6 %convert_reduce_fusion = (f32[1024]{0:T(1024)S(1)}, f32[1024]{0:T(1024)S(1)}) fusion(bf16[1024,512]{1,0:T(8,128)(2,1)} %all-gather.2.cloned.1.call-done), kind=kLoop, calls=%fused_computation.17 | loop fusion | flops 2095104 | bytes 1056768 | tf_op jit(solution)/shard_map/reduce_sum | solution.py:34
  30.1 1.7 %fusion.14 = bf16[1024,512]{1,0:T(8,128)(2,1)S(1)} fusion(bf16[1024,512]{1,0:T(8,128)(2,1)} %all-gather.2.cloned.1.call-done, f32[512]{0:T(512)S(1)} %bitcast.104, f32[512]{0:T(512)S(1)} %bitcast.103, f32[1024]{0:T(1024)S(1)} %get-tuple-element.45, f32[1024]{0:T(1024)S(1)} %get-tuple-element.44), kind=kLoop, calls=%fused_computation.22 | loop fusion | flops 3145728 | bytes 2109440 | tf_op jit(solution)/shard_map/convert_element_type | solution.py:106
  33.5 2.0 %gather_fusion = bf16[512,512]{1,0:T(8,128)(2,1)S(1)} fusion(bf16[1024,512]{1,0:T(8,128)(2,1)S(1)} %convolution_convert_fusion, s32[1024]{0:T(1024)S(1)} %pad_clamp_fusion.1), kind=kCustom, calls=%fused_computation | custom fusion | bytes 1050624 | tf_op jit(solution)/shard_map/jit(_take)/gather | solution.py:116
  35.7 3.4 %collective-permute-start = (bf16[256,512]{1,0:T(8,128)(2,1)S(1)}, bf16[256,512]{1,0:T(8,128)(2,1)S(1)}, u32[]{:S(2)}, u32[]{:S(2)}) collective-permute-start(bf16[256,512]{1,0:T(8,128)(2,1)S(1)} %get-tuple-element.34), channel_id=1, source_target_pairs={{0,4},{4,8},{8,12},{1,5},{5,9},{9,13},{2,6},{6,10},{10,14},{3,7},{... | collective-permute-start | bytes 786440 | tf_op jit(solution)/shard_map/ppermute | solution.py:27
  39.1 1.3 %collective-permute-start.1 = (bf16[256,512]{1,0:T(8,128)(2,1)S(1)}, bf16[256,512]{1,0:T(8,128)(2,1)}, u32[]{:S(2)}, u32[]{:S(2)}) collective-permute-start(bf16[256,512]{1,0:T(8,128)(2,1)S(1)} %get-tuple-element.35), channel_id=1, source_target_pairs={{4,0},{8,4},{12,8},{5,1},{9,5},{13,9},{6,2},{10,6},{14,10},{7,3},{... | collective-permute-start | bytes 786440 | tf_op jit(solution)/shard_map/ppermute | solution.py:28
  40.4 1.1 constant_dynamic-slice_fusion
  42.9 2.2 %collective-permute-done = bf16[256,512]{1,0:T(8,128)(2,1)S(1)} collective-permute-done((bf16[256,512]{1,0:T(8,128)(2,1)S(1)}, bf16[256,512]{1,0:T(8,128)(2,1)S(1)}, u32[]{:S(2)}, u32[]{:S(2)}) %collective-permute-start) | collective-permute-done | bytes 262176 | tf_op jit(solution)/shard_map/ppermute | solution.py:27
  45.7 3.5 %collective-permute-done.1 = bf16[256,512]{1,0:T(8,128)(2,1)} collective-permute-done((bf16[256,512]{1,0:T(8,128)(2,1)S(1)}, bf16[256,512]{1,0:T(8,128)(2,1)}, u32[]{:S(2)}, u32[]{:S(2)}) %collective-permute-start.1) | collective-permute-done | bytes 262176 | tf_op jit(solution)/shard_map/ppermute | solution.py:28
  49.3 1.5 %pad_maximum_fusion = bf16[1536,512]{1,0:T(8,128)(2,1)S(1)} fusion(bf16[256,512]{1,0:T(8,128)(2,1)} %collective-permute-done.1, bf16[256,512]{1,0:T(8,128)(2,1)} %copy-done.5, bf16[1024,512]{1,0:T(8,128)(2,1)} %copy-done.1), kind=kLoop, calls=%fused_computation.32 | loop fusion | flops 4718592 | bytes 3145728 | tf_op jit(solution)/shard_map/concatenate | solution.py:118
  50.8 5.0 %gather_fusion.1 = bf16[48,128,512]{2,1,0:T(8,128)(2,1)} fusion(bf16[12,128,512]{2,1,0:T(8,128)(2,1)S(1)} %bitcast.78, s32[1024]{0:T(1024)S(1)} %pad_clamp_fusion), kind=kCustom, calls=%fused_computation.1 | custom fusion | bytes 12583104 | tf_op jit(solution)/shard_map/while/body/eval_jaxpr/gather | solution.py:129
  55.7 8.6 %copy.27 = bf16[48,128,512]{1,2,0:T(8,128)(2,1)} copy(bf16[48,128,512]{2,1,0:T(8,128)(2,1)} %gather_fusion.1) | data formatting | bytes 12582912 | tf_op jit(solution)/shard_map/while/body/eval_jaxpr/gather | solution.py:129
  64.4 3.6 %fusion.56 = (bf16[4,12,128,256]{2,3,1,0:T(8,128)(2,1)S(1)}, bf16[4,12,128,256]{2,3,1,0:T(8,128)(2,1)S(1)}) fusion(bf16[4,12,128,512]{2,3,1,0:T(8,128)(2,1)} %bitcast.79), kind=kLoop, calls=%fused_computation.86 | loop fusion | bytes 12582912 | tf_op jit(solution)/shard_map/while/body/eval_jaxpr/slice | solution.py:133
  68.0 3.1 %select_reduce_fusion = (f32[4,4,128]{2,1,0:T(4,128)S(1)}, f32[4,4,128,12,128]{2,4,3,1,0:T(8,128)S(1)}) fusion(pred[4,128,12,128]{1,3,2,0:T(8,128)(4,1)S(1)} %bitcast.80, bf16[4,12,128,4,64]{2,4,3,1,0:T(8,128)(2,1)S(1)} %bitcast.84, bf16[4,128,4,64,1]{3,2,1,0,4:T(4,128)(2,1)S(1)} %bitcast.90), kind=kOutput, calls=%fused_computation.3 | convolution fusion | flops 412088320 | bytes 16785408 | tf_op jit(solution)/shard_map/while/body/eval_jaxpr/grhd,gtkhd->ghrtk/dot_general | solution.py:137
  71.1 2.8 %fusion = f32[4,4,128]{2,1,0:T(4,128)S(1)} fusion(f32[4,4,128,12,128]{2,4,3,1,0:T(8,128)S(1)} %get-tuple-element.49, f32[4,4,128]{2,1,0:T(4,128)S(1)} %get-tuple-element.48, pred[4,128,12,128]{1,3,2,0:T(8,128)(4,1)S(1)} %bitcast.81), kind=kLoop, calls=%fused_computation.4 | loop fusion | flops 12580864 | bytes 13385728 | tf_op jit(solution)/shard_map/while/body/eval_jaxpr/reduce_sum | solution.py:145
  74.0 3.4 %fusion.38 = bf16[4,128,4,64]{1,3,2,0:T(8,128)(2,1)S(1)} fusion(f32[4,4,128,12,128]{2,4,3,1,0:T(8,128)S(1)} %get-tuple-element.49, f32[4,4,128]{2,1,0:T(4,128)S(1)} %get-tuple-element.48, pred[4,128,12,128]{1,3,2,0:T(8,128)(4,1)S(1)} %bitcast.82, bf16[4,12,128,4,64]{2,4,3,1,0:T(8,128)(2,1)S(1)} %bitcast.83, f32[4,128,4]{1,2,0:T(4,128)S(1)} %bitcast.94), kind=kOutput, calls=%fused_computation.42 | convolution fusion | flops 415498240 | bytes 16793600 | tf_op jit(solution)/shard_map/while/body/eval_jaxpr/ghrtk,gtkhd->grhd/dot_general | solution.py:146
  77.8 7.6 %all_to_all.33 = bf16[2,256,256]{1,2,0:T(8,128)(2,1)S(1)} all-to-all(bf16[2,256,256]{1,2,0:T(8,128)(2,1)S(1)} %copy.34), channel_id=1, replica_groups=mesh['ens'=2,'space'=4,'chan'=2,'sub'=2] {'chan'}, dimensions={0} | all-to-all | bytes 524288 | tf_op jit(solution)/shard_map/all_to_all | solution.py:165
  85.4 1.4 %fusion.55 = (f32[256]{0:T(256)S(1)}, f32[256]{0:T(256)S(1)}, f32[256,512]{1,0:T(8,128)S(1)}) fusion(bf16[256,512]{0,1:T(8,128)(2,1)S(1)} %bitcast.89, bf16[512,512]{1,0:T(8,128)(2,1)S(1)} %copy-done.4, bf16[4,256,128]{2,1,0:T(8,128)(2,1)} %all-to-all-done), kind=kOutput, calls=%fused_computation.85 | convolution fusion | flops 134872576 | bytes 1574912 | tf_op jit(solution)/shard_map/dot_general | solution.py:164
  87.0 7.0 %all_gather.7 = bf16[512,512]{1,0:T(8,128)(2,1)S(1)} all-gather(bf16[256,512]{1,0:T(8,128)(2,1)S(1)} %add_convert_fusion), channel_id=1, replica_groups=mesh['ens'=2,'space'=4,'chan'=2,'sub'=2] {'chan'}, dimensions={0}, use_global_device_ids=true | all-gather | bytes 786432 | tf_op jit(solution)/shard_map/all_gather | solution.py:177
  94.0 2.3 %convolution_convert_fusion.1 = bf16[512,512]{1,0:T(8,128)(2,1)} fusion(bf16[1024,512]{1,0:T(8,128)(2,1)S(1)} %copy-done, bf16[512,512]{1,0:T(8,128)(2,1)S(1)} %all_gather.7, bf16[1024,512]{1,0:T(8,128)(2,1)S(1)} %copy-done.7), kind=kOutput, calls=%fused_computation.34 | convolution fusion | flops 1078722560 | bytes 3145728 | tf_op jit(solution)/shard_map/dot_general | solution.py:62
  96.3 13.8 %reduce-scatter.2.cloned.1.call-done = bf16[256,512]{1,0:T(8,128)(2,1)} async-done(((bf16[512,512]{1,0:T(8,128)(2,1)}), bf16[256,512]{1,0:T(8,128)(2,1)}) %reduce-scatter.2.cloned.1.call-update) | async-done | bytes 262160 | tf_op jit(solution)/shard_map/reduce_scatter | solution.py:178
  111.3 8.4 %all_to_all.34 = bf16[4,256,128]{2,1,0:T(8,128)(2,1)S(1)} all-to-all(bf16[4,256,128]{2,1,0:T(8,128)(2,1)S(1)} %pad_maximum_fusion.1), channel_id=1, replica_groups=mesh['ens'=2,'space'=4,'chan'=2,'sub'=2] {'chan','sub'}, dimensions={0} | all-to-all | bytes 524288 | tf_op jit(solution)/shard_map/all_to_all | solution.py:17
  (61 shorter events, 12.1 us)
Async XLA Ops:
  6.5 87.5 %copy-start = (bf16[1024,512]{1,0:T(8,128)(2,1)S(1)}, bf16[1024,512]{1,0:T(8,128)(2,1)}, u32[]{:S(2)}) copy-start(bf16[1024,512]{1,0:T(8,128)(2,1)} %param.21) | copy-start | bytes 3145732
  6.5 26.2 %copy-start.9 = (bf16[512,256]{1,0:T(8,128)(2,1)S(1)}, bf16[512,256]{1,0:T(8,128)(2,1)}, u32[]{:S(2)}) copy-start(bf16[512,256]{1,0:T(8,128)(2,1)} %param.17) | copy-start | bytes 786436
  6.5 26.2 %copy-start.8 = (bf16[512,256]{1,0:T(8,128)(2,1)S(1)}, bf16[512,256]{1,0:T(8,128)(2,1)}, u32[]{:S(2)}) copy-start(bf16[512,256]{1,0:T(8,128)(2,1)} %param.18) | copy-start | bytes 786436
  6.5 21.9 %all-gather.2.cloned.1.call-start = ((), (), s32[]{:S(2)}) async-start(), calls=%async_computation.4 | async-start | bytes 1310720 | tf_op jit(solution)/shard_map/all_gather | solution.py:105
  7.3 70.6 %all-to-all-start = ((bf16[4,256,128]{2,1,0:T(8,128)(2,1)}), bf16[4,256,128]{2,1,0:T(8,128)(2,1)}, u32[]{:S(2)}, u32[]{:S(2)}) async-start(bf16[4,256,128]{2,1,0:T(8,128)(2,1)} %bitcast.87), calls=%async_computation | async-start | bytes 524288 | tf_op jit(solution)/shard_map/all_to_all | solution.py:103
  11.5 98.6 %reduce-scatter.2.cloned.1.call-start = ((), (), s32[]{:S(2)}) async-start(), calls=%async_computation.5 | async-start | bytes 786432 | tf_op jit(solution)/shard_map/reduce_scatter | solution.py:178
  31.7 1.0 copy-start.2
  33.5 2.2 %copy-start.1 = (bf16[1024,512]{1,0:T(8,128)(2,1)}, bf16[1024,512]{1,0:T(8,128)(2,1)S(1)}, u32[]{:S(2)}) copy-start(bf16[1024,512]{1,0:T(8,128)(2,1)S(1)} %convolution_convert_fusion) | copy-start | bytes 3145732
  35.5 6.0 %copy-start.6 = (bf16[512,256]{1,0:T(8,128)(2,1)S(1)}, bf16[512,256]{1,0:T(8,128)(2,1)}, u32[]{:S(2)}) copy-start(bf16[512,256]{1,0:T(8,128)(2,1)} %param.16) | copy-start | bytes 786436
  35.7 9.3 %collective-permute-start = (bf16[256,512]{1,0:T(8,128)(2,1)S(1)}, bf16[256,512]{1,0:T(8,128)(2,1)S(1)}, u32[]{:S(2)}, u32[]{:S(2)}) collective-permute-start(bf16[256,512]{1,0:T(8,128)(2,1)S(1)} %get-tuple-element.34), channel_id=1, source_target_pairs={{0,4},{4,8},{8,12},{1,5},{5,9},{9,13},{2,6},{6,10},{10,14},{3,7},{... | collective-permute-start | bytes 786440 | tf_op jit(solution)/shard_map/ppermute | solution.py:27
  39.1 10.2 %collective-permute-start.1 = (bf16[256,512]{1,0:T(8,128)(2,1)S(1)}, bf16[256,512]{1,0:T(8,128)(2,1)}, u32[]{:S(2)}, u32[]{:S(2)}) collective-permute-start(bf16[256,512]{1,0:T(8,128)(2,1)S(1)} %get-tuple-element.35), channel_id=1, source_target_pairs={{4,0},{8,4},{12,8},{5,1},{9,5},{13,9},{6,2},{10,6},{14,10},{7,3},{... | collective-permute-start | bytes 786440 | tf_op jit(solution)/shard_map/ppermute | solution.py:28
  45.0 0.7 copy-start.5
  64.4 3.6 %copy-start.3 = (bf16[4,128,4,64]{3,2,1,0:T(4,128)(2,1)S(1)}, bf16[4,128,4,64]{3,2,1,0:T(4,128)(2,1)}, u32[]{:S(2)}) copy-start(bf16[4,128,4,64]{3,2,1,0:T(4,128)(2,1)} %reshape.236) | copy-start | bytes 786436
  73.9 11.5 %copy-start.4 = (bf16[512,512]{1,0:T(8,128)(2,1)S(1)}, bf16[512,512]{1,0:T(8,128)(2,1)}, u32[]{:S(2)}) copy-start(bf16[512,512]{1,0:T(8,128)(2,1)} %param.19) | copy-start | bytes 1572868
  77.4 16.6 %copy-start.7 = (bf16[1024,512]{1,0:T(8,128)(2,1)S(1)}, bf16[1024,512]{1,0:T(8,128)(2,1)}, u32[]{:S(2)}) copy-start(bf16[1024,512]{1,0:T(8,128)(2,1)} %param.20) | copy-start | bytes 3145732
Sparse Core Ops, SparseCore 0:
  8.9 19.5 all-gather.1
  96.4 13.6 reduce-scatter.1
